TPU v7x, 512 devices: a whole 4x4x16 slice. The times are simulated.
512 devices in a mesh: space: 128 (over z, x, core), rad: 4 (over y).
Axes of the slice: x: 4, y: 4, z: 16, core: 2. Of those that a mesh axis runs over, the one named last changes fastest.
Arguments:
- cell_bin: int32 [8388608], P(('space', 'rad')), may hold values from 0 to 255
- cell_fields: float32 [3, 8388608], P(None, ('space', 'rad')), may hold values from 0.0005 to 0.005
- tile_halo: int32 [65536], P(('space', 'rad')), may hold values from 0 to 4095, as said below
- halo_owner: int32 [4096], replicated, may hold values from 0 to 127, as said below
Outputs:
- enclosed_mass: float32 [4096, 256], P('space', 'rad')
- enclosed_volume: float32 [4096, 256], P('space', 'rad')
- cumulative_entropy: float32 [4096, 256], P('space', 'rad')
- circular_velocity: float32 [4096, 256], P('space', 'rad')
Inputs may be any that keep to these rules, and one draw needn't show every extreme that they name: `tile_halo`: the tiles of one device are in nondecreasing halo order; they go to exactly 64 owners, 2 tiles to each; the tiles of one device with one owner hold at most 1 distinct halos, and on every device some owner receives exactly 1. `halo_owner`: each index of space owns 32 consecutive halo ids.
All inputs are finite; a program needn't handle non-finite values.
Results may differ from a plain program's by a relative error of at most 0.000067.
Values sent between devices are 32-bit elements; how exact they have to be, the bound alone decides.
A program may use at most 64 MiB of HBM per device.

v0:
```python
import math

import jax
import jax.numpy as jnp
from jax import lax
from jax.sharding import PartitionSpec as P

TILE = 128
BINS = 256


log_inner = -2.302585092994046


def side_by_side(arrays, axis, split_dim, concat_dim, along):
    columns = [a.reshape(*a.shape[:along], -1) for a in arrays]
    both = jnp.concatenate(columns, axis=along)
    out, at, finished = (
        lax.all_to_all(both, axis, split_axis=split_dim, concat_axis=concat_dim, tiled=True),
        0,
        [],
    )
    for a, column in zip(arrays, columns):
        section = out[..., at : at + column.shape[along]]
        finished.append(section.reshape(*section.shape[:along], *a.shape[along:]))
        at += column.shape[along]
    return tuple(finished)


def cut_along(array, dim, devices):
    shape = array.shape
    pieces = array.reshape(*shape[:dim], devices, shape[dim] // devices, *shape[dim + 1 :])
    return jnp.moveaxis(pieces, dim, 0)


def summed_on_arrival(array, axis, dim):
    pieces = cut_along(array, dim, lax.axis_size(axis))
    arrived = lax.all_to_all(pieces, axis, split_axis=0, concat_axis=0, tiled=True)
    return arrived.sum(axis=0)


def in_order(pieces, dim):
    shape = list(pieces.shape[1:])
    shape[dim] *= pieces.shape[0]
    return jnp.moveaxis(pieces, 0, dim).reshape(shape)


def sent_to_all(array, axis):
    devices = lax.axis_size(axis)
    return lax.all_to_all(
        jnp.broadcast_to(array[None], (devices, *array.shape)), axis, 0, 0, tiled=True
    )


def gathered_copies(array, axis, dim):
    return in_order(sent_to_all(array, axis), dim)


def bin_tiles(cell_bin, cell_fields, tile_count):
    group_size = math.gcd(tile_count, 16)
    groups = tile_count // group_size
    bin_labels = cell_bin.reshape(groups, group_size, TILE)
    fields = cell_fields.reshape(3, groups, group_size, TILE).transpose(1, 0, 2, 3)
    bin_ids = jnp.arange(BINS, dtype=jnp.int32)

    def one_group(pair):
        labels, values = pair
        onehot = (labels[:, :, None] == bin_ids[None, None, :]).astype(jnp.float32)
        return jnp.einsum("ftc,tcb->tfb", values, onehot, precision=lax.Precision.HIGHEST)

    result = lax.map(one_group, (bin_labels, fields))
    return result.reshape(tile_count, 3 * BINS)


def pack_slots(pieces, target, slot_rank, slot_count, weights, spaces):
    slot_pos = target * slot_count + slot_rank
    placer = (
        slot_pos[:, None] == jnp.arange(spaces * slot_count, dtype=jnp.int32)[None, :]
    ).astype(jnp.float32)
    outgoing = jnp.dot(
        placer.T, pieces, precision=lax.Precision.HIGHEST, preferred_element_type=jnp.float32
    )
    slot_tags = (
        jnp.dot(
            weights, placer, precision=lax.Precision.HIGHEST, preferred_element_type=jnp.float32
        )
        - 1.0
    )
    return (outgoing.reshape(spaces, slot_count, 3 * BINS), slot_tags.reshape(spaces, slot_count))


def collect(received, got_tags, halo_dev, width):
    slot_rows = got_tags.size
    receiver = (
        got_tags.reshape(slot_rows)[:, None] == jnp.arange(halo_dev, dtype=jnp.float32)[None, :]
    ).astype(jnp.float32)
    return jnp.dot(
        receiver.T,
        received.reshape(slot_rows, width),
        precision=lax.Precision.HIGHEST,
        preferred_element_type=jnp.float32,
    )


def body(cell_bin, cell_fields, tile_halo, halo_owner):
    spaces = lax.axis_size("space")
    rads = lax.axis_size("rad")
    bin_dev = BINS // rads
    tile_count = tile_halo.shape[0]
    halo_dev = halo_owner.shape[0] // spaces
    capacity = max(2, 2 * tile_count // spaces)
    pieces = bin_tiles(cell_bin, cell_fields, tile_count)
    owner_hot = (halo_owner[:, None] == jnp.arange(spaces, dtype=jnp.int32)[None, :]).astype(
        jnp.int32
    )
    local_rank = jnp.sum((jnp.cumsum(owner_hot, axis=0) - owner_hot) * owner_hot, axis=1)
    target = halo_owner[tile_halo]
    labels = local_rank[tile_halo].astype(jnp.float32) + 1.0
    matches = (target[:, None] == target[None, :]).astype(jnp.int32)
    positions = jnp.arange(tile_count, dtype=jnp.int32)
    starts = jnp.concatenate(
        [jnp.ones((1,), jnp.int32), (tile_halo[1:] != tile_halo[:-1]).astype(jnp.int32)]
    )
    through = (positions[:, None] <= positions[None, :]).astype(jnp.int32)
    slot_rank = jnp.sum(matches * through * starts[:, None], axis=0) - 1
    slot_count = max(1, capacity // 2)
    outgoing, slot_tags = pack_slots(
        pieces, target, slot_rank, slot_count, labels * starts.astype(jnp.float32), spaces
    )
    received, got_tags = side_by_side((outgoing, slot_tags), "space", 0, 0, 2)
    owned = collect(received, got_tags, halo_dev, 3 * BINS)
    shares = summed_on_arrival(owned.reshape(halo_dev, 3, BINS), "rad", 2)
    running = jnp.cumsum(shares, axis=2)
    totals = running[:, :, -1]
    gathered = gathered_copies(totals[None], "rad", 0)
    before = (jnp.arange(rads, dtype=jnp.int32) < lax.axis_index("rad")).astype(jnp.float32)
    offset = jnp.sum(gathered * before[:, None, None], axis=0)
    running = running + offset[:, :, None]
    global_bin = lax.axis_index("rad") * bin_dev + jnp.arange(bin_dev, dtype=jnp.int32) + 1
    radius = jnp.exp(log_inner + global_bin.astype(jnp.float32) * (-log_inner / BINS))
    enclosed = running[:, 0, :]
    return (enclosed, running[:, 1, :], running[:, 2, :], jnp.sqrt(enclosed / radius[None, :]))


def solution(mesh):
    in_specs = (P(("space", "rad")), P(None, ("space", "rad")), P(("space", "rad")), P())
    out_specs = (P("space", "rad"), P("space", "rad"), P("space", "rad"), P("space", "rad"))
    return jax.shard_map(body, mesh=mesh, in_specs=in_specs, out_specs=out_specs, check_vma=False)
```

profile of v0, /device:TPU:32, one launch (start us, length us, event | category | flops | bytes accessed | tf_op | source)
XLA Modules:
  0.0 105.5 jit_solution(4290279782037807277)
XLA Ops:
  0.6 0.7 compare_select_fusion
  1.3 0.8 slice_compare_fusion
  2.1 1.6 %gather_fusion = s32[128]{0:T(128)S(1)} fusion(s32[4096]{0:T(1024)} %param.9, s32[1024]{0:T(1024)S(1)} %pad_clamp_fusion), kind=kCustom, calls=%fused_computation | custom fusion | bytes 1536 | tf_op jit(solution)/shard_map/gather | solution.py:117
  4.0 0.8 copy.29
  4.8 0.6 fusion.11
  5.5 0.2 broadcast_add_fusion
  5.7 1.2 %copy.30 = s32[128,32,128]{0,2,1:T(8,128)S(1)} copy(s32[128,32,128]{0,1,2:T(8,128)S(1)} %broadcast_add_fusion) | data formatting | bytes 4194304 | tf_op jit(solution)/shard_map/reduce_window_sum
  6.9 1.4 %fusion.10 = s32[4096]{0:T(1024)S(1)} fusion(s32[128,32,128]{0,2,1:T(8,128)S(1)} %copy.30, s32[4096]{0:T(1024)S(1)} %copy-done), kind=kLoop, calls=%fused_computation.14 | loop fusion | flops 2617344 | bytes 2129920 | tf_op jit(solution)/shard_map/reduce_sum | solution.py:116
  8.4 1.1 %gather_fusion.1 = s32[128]{0:T(128)S(1)} fusion(s32[4096]{0:T(1024)S(1)} %fusion.10, s32[1024]{0:T(1024)S(1)} %pad_clamp_fusion), kind=kCustom, calls=%fused_computation.1 | custom fusion | bytes 1536 | tf_op jit(solution)/shard_map/gather | solution.py:118
  9.5 0.2 fusion.14
  9.7 0.1 copy.31
  9.9 18.1 %while.11 = (s32[]{:T(128)}, f32[8,16,3,256]{3,2,1,0:T(4,128)S(1)}, f32[8,3,16,128]{3,1,2,0:T(4,128)}, s32[8,16,128]{2,1,0:T(8,128)}, s32[]{:T(128)}) while((s32[]{:T(128)}, f32[8,16,3,256]{3,2,1,0:T(4,128)S(1)}, f32[8,3,16,128]{3,1,2,0:T(4,128)}, s32[8,16,128]{2,1,0:T(8,128)}, s32[]{:T(128)}) %tuple.31), condition=%wide.region_2.3_spmd.clone, body=%wide.region_1.2_spmd.clone.sunk | while | flops 19398656 | bytes 123969 | solution.py:71
  9.9 0.7 dynamic-slice_bitcast_fusion.2
  10.6 1.6 %fusion.34 = f32[8,16,3,256]{3,2,1,0:T(4,128)S(1)} fusion(f32[8,16,3,256]{3,2,1,0:T(4,128)S(1)} %get-tuple-element.85, s32[]{:T(128)} %get-tuple-element.84, s32[16,128]{1,0:T(8,128)S(1)} %dynamic-slice_bitcast_fusion.2, f32[8,3,16,128]{3,1,2,0:T(4,128)} %get-tuple-element.91), kind=kOutput, calls=%fused_computation.6.clone.1 | convolution fusion | flops 19398656 | bytes 107520 | tf_op jit(solution)/shard_map/while/body/eval_jaxpr/ftc,tcb->tfb/dot_general | solution.py:69
  12.1 0.7 dynamic-slice_bitcast_fusion.2
  12.8 1.6 %fusion.34 = f32[8,16,3,256]{3,2,1,0:T(4,128)S(1)} fusion(f32[8,16,3,256]{3,2,1,0:T(4,128)S(1)} %get-tuple-element.85, s32[]{:T(128)} %get-tuple-element.84, s32[16,128]{1,0:T(8,128)S(1)} %dynamic-slice_bitcast_fusion.2, f32[8,3,16,128]{3,1,2,0:T(4,128)} %get-tuple-element.91), kind=kOutput, calls=%fused_computation.6.clone.1 | convolution fusion | flops 19398656 | bytes 107520 | tf_op jit(solution)/shard_map/while/body/eval_jaxpr/ftc,tcb->tfb/dot_general | solution.py:69
  14.4 0.7 dynamic-slice_bitcast_fusion.2
  15.1 1.6 %fusion.34 = f32[8,16,3,256]{3,2,1,0:T(4,128)S(1)} fusion(f32[8,16,3,256]{3,2,1,0:T(4,128)S(1)} %get-tuple-element.85, s32[]{:T(128)} %get-tuple-element.84, s32[16,128]{1,0:T(8,128)S(1)} %dynamic-slice_bitcast_fusion.2, f32[8,3,16,128]{3,1,2,0:T(4,128)} %get-tuple-element.91), kind=kOutput, calls=%fused_computation.6.clone.1 | convolution fusion | flops 19398656 | bytes 107520 | tf_op jit(solution)/shard_map/while/body/eval_jaxpr/ftc,tcb->tfb/dot_general | solution.py:69
  16.7 0.7 dynamic-slice_bitcast_fusion.2
  17.4 1.6 %fusion.34 = f32[8,16,3,256]{3,2,1,0:T(4,128)S(1)} fusion(f32[8,16,3,256]{3,2,1,0:T(4,128)S(1)} %get-tuple-element.85, s32[]{:T(128)} %get-tuple-element.84, s32[16,128]{1,0:T(8,128)S(1)} %dynamic-slice_bitcast_fusion.2, f32[8,3,16,128]{3,1,2,0:T(4,128)} %get-tuple-element.91), kind=kOutput, calls=%fused_computation.6.clone.1 | convolution fusion | flops 19398656 | bytes 107520 | tf_op jit(solution)/shard_map/while/body/eval_jaxpr/ftc,tcb->tfb/dot_general | solution.py:69
  18.9 0.7 dynamic-slice_bitcast_fusion.2
  19.6 1.6 %fusion.34 = f32[8,16,3,256]{3,2,1,0:T(4,128)S(1)} fusion(f32[8,16,3,256]{3,2,1,0:T(4,128)S(1)} %get-tuple-element.85, s32[]{:T(128)} %get-tuple-element.84, s32[16,128]{1,0:T(8,128)S(1)} %dynamic-slice_bitcast_fusion.2, f32[8,3,16,128]{3,1,2,0:T(4,128)} %get-tuple-element.91), kind=kOutput, calls=%fused_computation.6.clone.1 | convolution fusion | flops 19398656 | bytes 107520 | tf_op jit(solution)/shard_map/while/body/eval_jaxpr/ftc,tcb->tfb/dot_general | solution.py:69
  21.2 0.7 dynamic-slice_bitcast_fusion.2
  21.9 1.6 %fusion.34 = f32[8,16,3,256]{3,2,1,0:T(4,128)S(1)} fusion(f32[8,16,3,256]{3,2,1,0:T(4,128)S(1)} %get-tuple-element.85, s32[]{:T(128)} %get-tuple-element.84, s32[16,128]{1,0:T(8,128)S(1)} %dynamic-slice_bitcast_fusion.2, f32[8,3,16,128]{3,1,2,0:T(4,128)} %get-tuple-element.91), kind=kOutput, calls=%fused_computation.6.clone.1 | convolution fusion | flops 19398656 | bytes 107520 | tf_op jit(solution)/shard_map/while/body/eval_jaxpr/ftc,tcb->tfb/dot_general | solution.py:69
  23.4 0.7 dynamic-slice_bitcast_fusion.2
  24.1 1.6 %fusion.34 = f32[8,16,3,256]{3,2,1,0:T(4,128)S(1)} fusion(f32[8,16,3,256]{3,2,1,0:T(4,128)S(1)} %get-tuple-element.85, s32[]{:T(128)} %get-tuple-element.84, s32[16,128]{1,0:T(8,128)S(1)} %dynamic-slice_bitcast_fusion.2, f32[8,3,16,128]{3,1,2,0:T(4,128)} %get-tuple-element.91), kind=kOutput, calls=%fused_computation.6.clone.1 | convolution fusion | flops 19398656 | bytes 107520 | tf_op jit(solution)/shard_map/while/body/eval_jaxpr/ftc,tcb->tfb/dot_general | solution.py:69
  25.7 0.7 dynamic-slice_bitcast_fusion.2
  26.4 1.6 %fusion.34 = f32[8,16,3,256]{3,2,1,0:T(4,128)S(1)} fusion(f32[8,16,3,256]{3,2,1,0:T(4,128)S(1)} %get-tuple-element.85, s32[]{:T(128)} %get-tuple-element.84, s32[16,128]{1,0:T(8,128)S(1)} %dynamic-slice_bitcast_fusion.2, f32[8,3,16,128]{3,1,2,0:T(4,128)} %get-tuple-element.91), kind=kOutput, calls=%fused_computation.6.clone.1 | convolution fusion | flops 19398656 | bytes 107520 | tf_op jit(solution)/shard_map/while/body/eval_jaxpr/ftc,tcb->tfb/dot_general | solution.py:69
  28.0 0.4 convolution_bitcast_fusion
  28.5 1.2 %copy.32 = f32[128,1,769]{2,1,0:T(1,128)} copy(f32[128,1,769]{2,0,1:T(8,128)S(1)} %pad_maximum_fusion) | data formatting | bytes 787456 | tf_op jit(solution)/shard_map/concatenate | solution.py:17
  29.8 19.0 %all-to-all-start = ((f32[128,1,769]{2,1,0:T(1,128)}), f32[128,1,769]{2,1,0:T(1,128)S(1)}, u32[]{:S(2)}, u32[]{:S(2)}) async-start(f32[128,1,769]{2,1,0:T(1,128)} %copy.32), calls=%async_computation | async-start | bytes 917504 | tf_op jit(solution)/shard_map/all_to_all | solution.py:19
  48.8 30.5 %all-to-all-done = f32[128,1,769]{2,1,0:T(1,128)S(1)} async-done(((f32[128,1,769]{2,1,0:T(1,128)}), f32[128,1,769]{2,1,0:T(1,128)S(1)}, u32[]{:S(2)}, u32[]{:S(2)}) %all-to-all-start) | async-done | bytes 393760 | tf_op jit(solution)/shard_map/all_to_all | solution.py:19
  79.3 0.4 copy.37
  79.7 1.0 slice_reduce_fusion
  80.8 0.6 convolution_bitcast_fusion.1
  81.4 0.8 reshape.104
  82.2 4.5 %all-to-all-start.1 = ((f32[4,1,6144]{2,1,0:T(1,128)}), f32[4,1,6144]{2,1,0:T(1,128)S(1)}, u32[]{:S(2)}, u32[]{:S(2)}) async-start(f32[4,1,6144]{2,1,0:T(1,128)} %reshape.104), calls=%async_computation.1 | async-start | bytes 196608 | tf_op jit(solution)/shard_map/all_to_all | solution.py:38
  86.7 5.8 %all-to-all-done.1 = f32[4,1,6144]{2,1,0:T(1,128)S(1)} async-done(((f32[4,1,6144]{2,1,0:T(1,128)}), f32[4,1,6144]{2,1,0:T(1,128)S(1)}, u32[]{:S(2)}, u32[]{:S(2)}) %all-to-all-start.1) | async-done | bytes 98336 | tf_op jit(solution)/shard_map/all_to_all | solution.py:38
  92.5 0.5 broadcast.90
  93.0 0.9 reduce.4
  93.9 0.2 reshape.105
  94.1 0.7 reduce_window_sum.28
  94.8 0.2 slice_reduce_fusion.1
  94.9 0.6 broadcast_in_dim.17
  95.5 3.2 %all-to-all-start.2 = ((f32[4,1,32,3]{2,1,3,0:T(1,128)}), f32[4,1,32,3]{2,1,3,0:T(1,128)S(1)}, u32[]{:S(2)}, u32[]{:S(2)}) async-start(f32[4,1,32,3]{2,1,3,0:T(1,128)} %broadcast_in_dim.17), calls=%async_computation.2 | async-start | bytes 12288 | tf_op jit(solution)/shard_map/all_to_all | solution.py:50
  98.8 5.3 %all-to-all-done.2 = f32[4,1,32,3]{2,1,3,0:T(1,128)S(1)} async-done(((f32[4,1,32,3]{2,1,3,0:T(1,128)}), f32[4,1,32,3]{2,1,3,0:T(1,128)S(1)}, u32[]{:S(2)}, u32[]{:S(2)}) %all-to-all-start.2) | async-done | bytes 1568 | tf_op jit(solution)/shard_map/all_to_all | solution.py:50
  104.2 0.6 slice_bitcast_fusion
  104.8 0.6 divide_sqrt_fusion
  (19 shorter events, 0.7 us)
Async XLA Ops:
  5.7 1.2 %copy-start = (s32[4096]{0:T(1024)S(1)}, s32[4096]{0:T(1024)}, u32[]{:S(2)}) copy-start(s32[4096]{0:T(1024)} %param.9) | copy-start | bytes 49156
  29.8 49.5 %all-to-all-start = ((f32[128,1,769]{2,1,0:T(1,128)}), f32[128,1,769]{2,1,0:T(1,128)S(1)}, u32[]{:S(2)}, u32[]{:S(2)}) async-start(f32[128,1,769]{2,1,0:T(1,128)} %copy.32), calls=%async_computation | async-start | bytes 917504 | tf_op jit(solution)/shard_map/all_to_all | solution.py:19
  82.2 10.3 %all-to-all-start.1 = ((f32[4,1,6144]{2,1,0:T(1,128)}), f32[4,1,6144]{2,1,0:T(1,128)S(1)}, u32[]{:S(2)}, u32[]{:S(2)}) async-start(f32[4,1,6144]{2,1,0:T(1,128)} %reshape.104), calls=%async_computation.1 | async-start | bytes 196608 | tf_op jit(solution)/shard_map/all_to_all | solution.py:38
  95.5 8.5 %all-to-all-start.2 = ((f32[4,1,32,3]{2,1,3,0:T(1,128)}), f32[4,1,32,3]{2,1,3,0:T(1,128)S(1)}, u32[]{:S(2)}, u32[]{:S(2)}) async-start(f32[4,1,32,3]{2,1,3,0:T(1,128)} %broadcast_in_dim.17), calls=%async_computation.2 | async-start | bytes 12288 | tf_op jit(solution)/shard_map/all_to_all | solution.py:50
where the time goes:
time: 107 us; the launch traced here: 105 us
  waiting for transfers between devices  41.5 us (39%)
  starting transfers between devices  26.7 us (25%)
  local copies, waits for them, and re-layouts  16.3 us (15%)
  matrix products  13.7 us (13%)
  other arithmetic  6.44 us (6%)
    all_to_all x1, waiting for transfers between devices, side_by_side(): lax.all_to_all(both, axis, split_axis=split_dim, concat_axis=concat_dim,...  30.5 us
    all_to_all x1, starting transfers between devices, side_by_side(): lax.all_to_all(both, axis, split_axis=split_dim, concat_axis=concat_dim,...  19 us
    dot_general x8, matrix products, one_group(): jnp.einsum('ftc,tcb->tfb', values, onehot, precision=lax.Precision.HIGHEST)  12.4 us
    all_to_all x1, waiting for transfers between devices, summed_on_arrival(): lax.all_to_all(pieces, axis, split_axis=0, concat_axis=0, tiled=True)  5.8 us
    eq x8, local copies, waits for them, and re-layouts, one_group(): onehot = (labels[:, :, None] == bin_ids[None, None, :]).astype(jnp.float32)  5.65 us
    all_to_all x1, waiting for transfers between devices, sent_to_all(): lax.all_to_all(jnp.broadcast_to(array[None], (devices, *array.shape)), ax...  5.25 us
    all_to_all x1, starting transfers between devices, summed_on_arrival(): lax.all_to_all(pieces, axis, split_axis=0, concat_axis=0, tiled=True)  4.46 us
    all_to_all x1, starting transfers between devices, sent_to_all(): lax.all_to_all(jnp.broadcast_to(array[None], (devices, *array.shape)), ax...  3.25 us
  transfers between devices with their start and end apart: 3, of which 3 were waited for; matrix products, arithmetic and copies ran while one was open for 0% of the time, Pallas kernels for 0%

commit v1 on v0

v1 whole, which is shorter than its diff:
```python
import functools

import jax
import jax.numpy as jnp
from jax import lax
from jax.experimental import pallas as pl
from jax.experimental.pallas import tpu as pltpu
from jax.sharding import PartitionSpec as P

MESH = pl.DeviceIdType.MESH
F32 = jnp.float32
BF16 = jnp.bfloat16
TILE = 128
BINS = 256
QUARTER = 64
HALO_DEV = 32
log_inner = -2.302585092994046


def split3(v):
    high = v.astype(BF16)
    rest = v - high.astype(F32)
    mid = rest.astype(BF16)
    low = (rest - mid.astype(F32)).astype(BF16)
    return high, mid, low


def iota(shape, dim):
    return lax.broadcasted_iota(jnp.int32, shape, dim)


def nt(a, b):
    return lax.dot_general(a, b, (((1,), (1,)), ((), ())), preferred_element_type=F32)


def bin_piece(k, bin_ref, fld_ref):
    label = jnp.concatenate([bin_ref[pl.ds(2 * k, 1), :], bin_ref[pl.ds(2 * k + 1, 1), :]], axis=1)
    low = label & (QUARTER - 1)
    high = lax.shift_right_logical(label, 6)
    v = fld_ref[:, pl.ds(pl.multiple_of(2 * TILE * k, 2 * TILE), 2 * TILE)]
    pad = jnp.zeros((1, 2 * TILE), F32)
    v8 = jnp.concatenate([v, pad, v, pad], axis=0)
    row = iota((8, 2 * TILE), 0)
    parts = [[], [], []]
    bases = []
    for t in range(2):
        quarter = 2 * t + lax.shift_right_logical(row, 2)
        own = jnp.where(high == quarter, v8, 0.0)
        for s, part in enumerate(split3(own)):
            parts[s].append(part)
        bases.append(jnp.sum(jnp.where(high < quarter, v8, 0.0), axis=1, keepdims=True))
    lhs = jnp.concatenate(parts[0] + parts[1] + parts[2], axis=0)
    below = jnp.where(low <= iota((QUARTER, 2 * TILE), 0), 1.0, 0.0).astype(BF16)
    below = jnp.concatenate([below, below], axis=0)
    out = nt(lhs, below)
    out = out[0:16] + out[16:32] + out[32:48]
    return out + jnp.concatenate(bases, axis=0)


def kernel(na, nj, ny, halo_ref, owner_ref, bin_ref, fld_ref, mass_ref, vol_ref, ent_ref, vel_ref,
           pieces, code_v, code_s, send, recv, dense, got, code_sem, send1, recv1, send2, recv2):
    owners = na * nj
    count = owners // 2
    pairs = na // 2
    group = nj * ny
    rows = 3 * pairs + 1
    space = lax.axis_index("space")
    y = lax.axis_index("rad")
    a = space // nj
    j = space % nj
    me = j * ny + y

    barrier = pltpu.get_barrier_semaphore()

    def greet(i, carry):
        t = lax.rem(me + i, group)
        pl.semaphore_signal(barrier, inc=1, device_id=(a * nj + t // ny, lax.rem(t, ny)), device_id_type=MESH)
        return carry

    for i in range(1, na):
        pl.semaphore_signal(barrier, inc=1, device_id=(lax.rem(a + i, na) * nj + j, y), device_id_type=MESH)
    lax.fori_loop(1, group, greet, 0)

    lane = iota((8, owners), 1)

    def note(k, codes):
        halo = halo_ref[2 * k]
        code = 1 + HALO_DEV * k + (halo & (HALO_DEV - 1))
        return jnp.where(lane == owner_ref[halo], code, codes)

    code_v[...] = lax.fori_loop(0, count, note, jnp.zeros((8, owners), jnp.int32), unroll=min(8, count))
    noting = pltpu.make_async_copy(code_v, code_s, code_sem)
    noting.start()

    def one_piece(k, carry):
        pieces[k] = bin_piece(k, bin_ref, fld_ref)
        return carry

    lax.fori_loop(0, count, one_piece, 0, unroll=min(4, count))
    noting.wait()
    pl.semaphore_wait(barrier, group - 1 + na - 1)

    lane128 = iota((1, 128), 1)
    left = iota((16, 128), 1) < QUARTER
    tag = 128 // na

    def outbound(dj, dy):
        t = dj * ny + dy
        return pltpu.make_async_remote_copy(
            src_ref=send.at[t], dst_ref=recv.at[me], send_sem=send1.at[t], recv_sem=recv1.at[me],
            device_id=(a * nj + dj, dy), device_id_type=MESH)

    def assemble(i, carry):
        dj = lax.rem(j + 1 + i, nj)
        labels = jnp.zeros((1, 128), F32)
        for p in range(pairs):
            codes = [code_s[0, 2 * p * nj + dj], code_s[0, (2 * p + 1) * nj + dj]]
            held = [pieces[lax.shift_right_logical(jnp.maximum(c - 1, 0), 5)] for c in codes]
            there = [jnp.where(c > 0, 1, 0) for c in codes]
            both = jnp.where(left, held[0], held[1])
            both = jnp.where(jnp.where(left, there[0], there[1]) > 0, both, 0.0)
            for par in range(2):
                rank = jnp.where(codes[par] > 0, (codes[par] - 1) & (HALO_DEV - 1), -1).astype(F32)
                labels = jnp.where(lane128 // tag == 2 * p + par, rank, labels)
            for q in range(ny):
                send[dj * ny + q, 3 * p:3 * p + 3, :] = both[4 * q:4 * q + 3]
        for q in range(ny):
            send[dj * ny + q, rows - 1:rows, :] = labels
        for dy in range(ny):
            @pl.when(jnp.logical_or(dj != j, dy != y))
            def _():
                outbound(dj, dy).start()
        return carry

    lax.fori_loop(0, nj, assemble, 0)
    recv[me] = send[me]

    def inbound(t):
        return pltpu.make_async_remote_copy(
            src_ref=send.at[t], dst_ref=recv.at[t], send_sem=send1.at[t], recv_sem=recv1.at[t],
            device_id=(a * nj + t // ny, lax.rem(t, ny)), device_id_type=MESH)

    def arrive(i, carry):
        inbound(lax.rem(me + group - i, group)).wait_recv()
        return carry

    lax.fori_loop(1, group, arrive, 0)

    labels = recv[:, rows - 1, :].astype(BF16)
    labels = jnp.concatenate([labels] * 3, axis=0)
    spread = jnp.where(iota((na * HALO_DEV, 128), 1) == tag * (iota((na * HALO_DEV, 128), 0) // HALO_DEV), 1.0, 0.0).astype(BF16)
    spread = nt(spread, labels)
    wanted = (iota(spread.shape, 0) & (HALO_DEV - 1)).astype(F32)
    chosen = jnp.where(spread == wanted, 1.0, 0.0).astype(BF16)

    def onward(d):
        return pltpu.make_async_remote_copy(
            src_ref=dense.at[d], dst_ref=got.at[a], send_sem=send2.at[d], recv_sem=recv2.at[a],
            device_id=(d * nj + j, y), device_id_type=MESH)

    for p in range(pairs):
        columns = [jnp.concatenate(split3(recv[:, 3 * p + f, :]), axis=0) for f in range(3)]
        total = jnp.dot(chosen[2 * HALO_DEV * p:2 * HALO_DEV * (p + 1)], jnp.concatenate(columns, axis=1),
                        preferred_element_type=F32)
        for par in range(2):
            d = 2 * p + par
            for f in range(3):
                top = total[32 * par:32 * par + 16, 128 * f:128 * f + 128]
                bottom = total[32 * par + 16:32 * par + 32, 128 * f:128 * f + 128]
                if par == 0:
                    merged = jnp.where(left, top, pltpu.roll(bottom, QUARTER, 1))
                else:
                    merged = jnp.where(left, pltpu.roll(top, QUARTER, 1), bottom)
                dense[d, :, 128 * f:128 * f + 128] = merged

            @pl.when(d != a)
            def _():
                onward(d).start()

    total = dense[a]

    for i in range(1, na):
        t = lax.rem(a + i, na)
        pltpu.make_async_remote_copy(
            src_ref=dense.at[t], dst_ref=got.at[t], send_sem=send2.at[t], recv_sem=recv2.at[t],
            device_id=(t * nj + j, y), device_id_type=MESH).wait_recv()
        total = total + got[t]

    bins = (y * QUARTER + 1 + iota((16, QUARTER), 1)).astype(F32)
    radius = jnp.exp(log_inner + bins * (-log_inner / BINS))
    for f, ref in enumerate((mass_ref, vol_ref, ent_ref)):
        block = total[:, 128 * f:128 * f + 128]
        for half, part in enumerate((block, pltpu.roll(block, QUARTER, 1))):
            part = part[:, :QUARTER]
            ref[16 * half:16 * half + 16, :] = part
            if f == 0:
                vel_ref[16 * half:16 * half + 16, :] = jnp.sqrt(part / radius)

    def sent(i, carry):
        inbound(lax.rem(me + i, group)).wait_send()
        return carry

    lax.fori_loop(1, group, sent, 0)
    for i in range(1, na):
        onward(lax.rem(a + i, na)).wait_send()


def solution(mesh):
    spaces, ny = mesh.shape["space"], mesh.shape["rad"]
    na = 8 if spaces == 128 else 2
    nj = spaces // na
    group, rows = nj * ny, 3 * (na // 2) + 1

    def body(cell_bin, cell_fields, tile_halo, halo_owner):
        smem = pl.BlockSpec(memory_space=pltpu.SMEM)
        vmem = pl.BlockSpec(memory_space=pltpu.VMEM)
        dma = pltpu.SemaphoreType.DMA
        out = jax.ShapeDtypeStruct((HALO_DEV, QUARTER), F32)
        return pl.pallas_call(
            functools.partial(kernel, na, nj, ny),
            out_shape=(out,) * 4,
            in_specs=[smem, smem, vmem, vmem],
            out_specs=(vmem,) * 4,
            scratch_shapes=[
                pltpu.VMEM((spaces // 2, 16, 128), F32),
                pltpu.VMEM((8, spaces), jnp.int32),
                pltpu.SMEM((8, spaces), jnp.int32),
                pltpu.VMEM((group, rows, 128), F32),
                pltpu.VMEM((group, rows, 128), F32),
                pltpu.VMEM((na, 16, 384), F32),
                pltpu.VMEM((na, 16, 384), F32),
                dma, dma((group,)), dma((group,)), dma((na,)), dma((na,)),
            ],
            compiler_params=pltpu.CompilerParams(collective_id=0, has_side_effects=True),
            name="profiles",
        )(tile_halo, halo_owner, cell_bin.reshape(-1, TILE), cell_fields)

    in_specs = (P(("space", "rad")), P(None, ("space", "rad")), P(("space", "rad")), P())
    out_specs = (P("space", "rad"),) * 4
    return jax.shard_map(body, mesh=mesh, in_specs=in_specs, out_specs=out_specs, check_vma=False)
```

time: 107 us -> 44.3 us (0.41)
  the two profiles are of different devices: /device:TPU:32 before, /device:TPU:64 now
where the time goes in v1:
time: 44.3 us; the launch traced here: 43.9 us
  Pallas kernels  39.8 us (90%)
  local copies, waits for them, and re-layouts  3.39 us (8%)
  between operations  0.65 us (1%)
    pallas_call x1, Pallas kernels, body(): pl.pallas_call(functools.partial(kernel, na, nj, ny), out_shape=(out,) *...  39.8 us
    unnamed x10, local copies, waits for them, and re-layouts  3.39 us

profile of v1, /device:TPU:64, one launch (start us, length us, event | category | flops | bytes accessed | tf_op | source)
XLA Modules:
  0.0 43.9 jit_solution(5216626054637609295)
XLA Ops:
  0.6 39.8 %profiles.1 = (f32[32,64]{1,0:T(8,128)}, f32[32,64]{1,0:T(8,128)}, f32[32,64]{1,0:T(8,128)}, f32[32,64]{1,0:T(8,128)}) custom-call(s32[128]{0:T(128)} %halo_ref.1, s32[4096]{0:T(1024)} %owner_ref.1, s32[128,128]{1,0:T(8,128)} %bitcast.1, f32[3,16384]{1,0:T(4,128)} %fld_ref.1), custom_call_target="tpu_custom_call" | custom-call | tf_op jit(solution)/shard_map/profiles/pallas_call | solution.py:219
  40.5 0.0 copy-start.2
  40.5 1.3 %copy.12 = f32[32,64]{1,0:T(8,128)} copy(f32[32,64]{1,0:T(8,128)} %get-tuple-element.8) | data formatting | bytes 16384
  41.8 0.0 copy-done.2
  41.8 0.0 copy-start.1
  41.8 0.6 %copy.13 = f32[32,64]{1,0:T(8,128)} copy(f32[32,64]{1,0:T(8,128)S(1)} %copy-done.2) | data formatting | bytes 16384
  42.4 0.1 copy-done.1
  42.5 0.0 copy-start
  42.5 0.6 %copy.14 = f32[32,64]{1,0:T(8,128)} copy(f32[32,64]{1,0:T(8,128)S(1)} %copy-done.1) | data formatting | bytes 16384
  43.1 0.1 copy-done
  43.3 0.6 %copy.15 = f32[32,64]{1,0:T(8,128)} copy(f32[32,64]{1,0:T(8,128)S(1)} %copy-done) | data formatting | bytes 16384
Async XLA Ops:
  40.5 1.3 %copy-start.2 = (f32[32,64]{1,0:T(8,128)S(1)}, f32[32,64]{1,0:T(8,128)}, u32[]{:S(2)}) copy-start(f32[32,64]{1,0:T(8,128)} %get-tuple-element.9) | copy-start | bytes 24580
  41.8 0.7 %copy-start.1 = (f32[32,64]{1,0:T(8,128)S(1)}, f32[32,64]{1,0:T(8,128)}, u32[]{:S(2)}) copy-start(f32[32,64]{1,0:T(8,128)} %get-tuple-element.10) | copy-start | bytes 24580
  42.5 0.7 %copy-start = (f32[32,64]{1,0:T(8,128)S(1)}, f32[32,64]{1,0:T(8,128)}, u32[]{:S(2)}) copy-start(f32[32,64]{1,0:T(8,128)} %get-tuple-element.11) | copy-start | bytes 24580

commit v2 on v1

--- a/solution.py
+++ b/solution.py
@@ -57,8 +57,8 @@
     return out + jnp.concatenate(bases, axis=0)
 
 
-def kernel(na, nj, ny, halo_ref, owner_ref, bin_ref, fld_ref, mass_ref, vol_ref, ent_ref, vel_ref,
-           pieces, code_v, code_s, send, recv, dense, got, code_sem, send1, recv1, send2, recv2):
+def kernel(na, nj, ny, halo_hbm, owner_hbm, bin_hbm, fld_hbm, got, halo_ref, owner_ref, bin_ref, fld_ref,
+           pieces, code_v, code_s, send, recv, dense, in_sem, code_sem, send1, recv1, send2, recv2, own_sem):
     owners = na * nj
     count = owners // 2
     pairs = na // 2
@@ -70,16 +70,26 @@
     j = space % nj
     me = j * ny + y
 
+    chunks = min(4, count)
+    size = count // chunks
+    fetches = [pltpu.make_async_copy(halo_hbm, halo_ref, in_sem.at[0]),
+               pltpu.make_async_copy(owner_hbm, owner_ref, in_sem.at[1])]
+    for c in range(chunks):
+        fetches.append(pltpu.make_async_copy(
+            bin_hbm.at[2 * size * c:2 * size * (c + 1)], bin_ref.at[2 * size * c:2 * size * (c + 1)], in_sem.at[2 + 2 * c]))
+        cells = slice(2 * TILE * size * c, 2 * TILE * size * (c + 1))
+        fetches.append(pltpu.make_async_copy(fld_hbm.at[:, cells], fld_ref.at[:, cells], in_sem.at[3 + 2 * c]))
+    for fetch in fetches:
+        fetch.start()
+
     barrier = pltpu.get_barrier_semaphore()
-
-    def greet(i, carry):
-        t = lax.rem(me + i, group)
-        pl.semaphore_signal(barrier, inc=1, device_id=(a * nj + t // ny, lax.rem(t, ny)), device_id_type=MESH)
-        return carry
-
     for i in range(1, na):
         pl.semaphore_signal(barrier, inc=1, device_id=(lax.rem(a + i, na) * nj + j, y), device_id_type=MESH)
-    lax.fori_loop(1, group, greet, 0)
+    for dj in range(nj):
+        for dy in range(ny):
+            @pl.when(jnp.logical_or(dj != j, dy != y))
+            def _():
+                pl.semaphore_signal(barrier, inc=1, device_id=(a * nj + dj, dy), device_id_type=MESH)
 
     lane = iota((8, owners), 1)
 
@@ -88,15 +98,28 @@
         code = 1 + HALO_DEV * k + (halo & (HALO_DEV - 1))
         return jnp.where(lane == owner_ref[halo], code, codes)
 
-    code_v[...] = lax.fori_loop(0, count, note, jnp.zeros((8, owners), jnp.int32), unroll=min(8, count))
-    noting = pltpu.make_async_copy(code_v, code_s, code_sem)
-    noting.start()
+    def piece_and_notes(k, codes):
+        pieces[k] = bin_piece(k, bin_ref, fld_ref)
+        return note(2 * k + 1, note(2 * k, codes))
 
     def one_piece(k, carry):
         pieces[k] = bin_piece(k, bin_ref, fld_ref)
         return carry
 
-    lax.fori_loop(0, count, one_piece, 0, unroll=min(4, count))
+    noting = pltpu.make_async_copy(code_v, code_s, code_sem)
+    fetches[0].wait()
+    fetches[1].wait()
+    codes = jnp.zeros((8, owners), jnp.int32)
+    for c in range(chunks):
+        fetches[2 + 2 * c].wait()
+        fetches[3 + 2 * c].wait()
+        if 2 * c < chunks:
+            codes = lax.fori_loop(size * c, size * (c + 1), piece_and_notes, codes, unroll=size)
+            if 2 * (c + 1) == chunks:
+                code_v[...] = codes
+                noting.start()
+        else:
+            lax.fori_loop(size * c, size * (c + 1), one_piece, 0, unroll=size)
     noting.wait()
     pl.semaphore_wait(barrier, group - 1 + na - 1)
 
@@ -177,16 +200,29 @@
             def _():
                 onward(d).start()
 
-    total = dense[a]
-
+    keep = pltpu.make_async_copy(dense.at[a], got.at[a], own_sem)
+    keep.start()
     for i in range(1, na):
         t = lax.rem(a + i, na)
         pltpu.make_async_remote_copy(
             src_ref=dense.at[t], dst_ref=got.at[t], send_sem=send2.at[t], recv_sem=recv2.at[t],
             device_id=(t * nj + j, y), device_id_type=MESH).wait_recv()
-        total = total + got[t]
-
-    bins = (y * QUARTER + 1 + iota((16, QUARTER), 1)).astype(F32)
+    keep.wait()
+
+    def sent(i, carry):
+        inbound(lax.rem(me + i, group)).wait_send()
+        return carry
+
+    lax.fori_loop(1, group, sent, 0)
+    for i in range(1, na):
+        onward(lax.rem(a + i, na)).wait_send()
+
+
+def finish(na, got_ref, mass_ref, vol_ref, ent_ref, vel_ref):
+    total = got_ref[0]
+    for t in range(1, na):
+        total = total + got_ref[t]
+    bins = (lax.axis_index("rad") * QUARTER + 1 + iota((16, QUARTER), 1)).astype(F32)
     radius = jnp.exp(log_inner + bins * (-log_inner / BINS))
     for f, ref in enumerate((mass_ref, vol_ref, ent_ref)):
         block = total[:, 128 * f:128 * f + 128]
@@ -196,14 +232,6 @@
             if f == 0:
                 vel_ref[16 * half:16 * half + 16, :] = jnp.sqrt(part / radius)
 
-    def sent(i, carry):
-        inbound(lax.rem(me + i, group)).wait_send()
-        return carry
-
-    lax.fori_loop(1, group, sent, 0)
-    for i in range(1, na):
-        onward(lax.rem(a + i, na)).wait_send()
-
 
 def solution(mesh):
     spaces, ny = mesh.shape["space"], mesh.shape["rad"]
@@ -212,28 +240,34 @@
     group, rows = nj * ny, 3 * (na // 2) + 1
 
     def body(cell_bin, cell_fields, tile_halo, halo_owner):
-        smem = pl.BlockSpec(memory_space=pltpu.SMEM)
         vmem = pl.BlockSpec(memory_space=pltpu.VMEM)
+        anywhere = pl.BlockSpec(memory_space=pl.ANY)
         dma = pltpu.SemaphoreType.DMA
         out = jax.ShapeDtypeStruct((HALO_DEV, QUARTER), F32)
-        return pl.pallas_call(
+        got = pl.pallas_call(
             functools.partial(kernel, na, nj, ny),
-            out_shape=(out,) * 4,
-            in_specs=[smem, smem, vmem, vmem],
-            out_specs=(vmem,) * 4,
+            out_shape=jax.ShapeDtypeStruct((na, 16, 384), F32),
+            in_specs=[anywhere] * 4,
+            out_specs=anywhere,
             scratch_shapes=[
+                pltpu.SMEM(tile_halo.shape, jnp.int32),
+                pltpu.SMEM(halo_owner.shape, jnp.int32),
+                pltpu.VMEM((tile_halo.shape[0], TILE), jnp.int32),
+                pltpu.VMEM(cell_fields.shape, F32),
                 pltpu.VMEM((spaces // 2, 16, 128), F32),
                 pltpu.VMEM((8, spaces), jnp.int32),
                 pltpu.SMEM((8, spaces), jnp.int32),
                 pltpu.VMEM((group, rows, 128), F32),
                 pltpu.VMEM((group, rows, 128), F32),
                 pltpu.VMEM((na, 16, 384), F32),
-                pltpu.VMEM((na, 16, 384), F32),
-                dma, dma((group,)), dma((group,)), dma((na,)), dma((na,)),
+                dma((10,)), dma, dma((group,)), dma((group,)), dma((na,)), dma((na,)), dma,
             ],
             compiler_params=pltpu.CompilerParams(collective_id=0, has_side_effects=True),
             name="profiles",
         )(tile_halo, halo_owner, cell_bin.reshape(-1, TILE), cell_fields)
+        return pl.pallas_call(
+            functools.partial(finish, na), out_shape=(out,) * 4, in_specs=[vmem], out_specs=(vmem,) * 4, name="finish",
+        )(got)
 
     in_specs = (P(("space", "rad")), P(None, ("space", "rad")), P(("space", "rad")), P())
     out_specs = (P("space", "rad"),) * 4

time: 44.3 us -> 40.7 us (0.919)
  the two profiles are of different devices: /device:TPU:64 before, /device:TPU:8 now
where the time goes in v2:
time: 40.7 us; the launch traced here: 40.5 us
  Pallas kernels  39.9 us (98%)
  between operations  0.64 us (2%)
    pallas_call x1, Pallas kernels, body(): pl.pallas_call(functools.partial(kernel, na, nj, ny), out_shape=jax.Shape...  38.2 us
    pallas_call x1, Pallas kernels, body(): pl.pallas_call(functools.partial(finish, na), out_shape=(out,) * 4, in_sp...  1.63 us

profile of v2, /device:TPU:8, one launch (start us, length us, event | category | flops | bytes accessed | tf_op | source)
XLA Modules:
  0.0 40.5 jit_solution(13886525962631236648)
XLA Ops:
  0.6 38.2 %profiles.1.got_ref = f32[8,16,384]{2,1,0:T(8,128)} custom-call(s32[128]{0:T(128)} %halo_hbm.1, s32[4096]{0:T(1024)} %owner_hbm.1, s32[128,128]{1,0:T(8,128)} %bitcast.1, f32[3,16384]{1,0:T(4,128)} %fld_hbm.1), custom_call_target="tpu_custom_call" | custom-call | tf_op jit(solution)/shard_map/profiles/pallas_call | solution.py:247
  38.9 1.6 %finish.1 = (f32[32,64]{1,0:T(8,128)}, f32[32,64]{1,0:T(8,128)}, f32[32,64]{1,0:T(8,128)}, f32[32,64]{1,0:T(8,128)}) custom-call(f32[8,16,384]{2,1,0:T(8,128)} %profiles.1.got_ref), custom_call_target="tpu_custom_call" | custom-call | tf_op jit(solution)/shard_map/finish/pallas_call | solution.py:268

commit v3 on v2

--- a/solution.py
+++ b/solution.py
@@ -58,12 +58,11 @@
 
 
 def kernel(na, nj, ny, halo_hbm, owner_hbm, bin_hbm, fld_hbm, got, halo_ref, owner_ref, bin_ref, fld_ref,
-           pieces, code_v, code_s, send, recv, dense, in_sem, code_sem, send1, recv1, send2, recv2, own_sem):
+           pieces, code_v, code_s, send, recv, dense, in_sem, code_sem, send1, recv1, send2, recv2):
     owners = na * nj
     count = owners // 2
     pairs = na // 2
     group = nj * ny
-    rows = 3 * pairs + 1
     space = lax.axis_index("space")
     y = lax.axis_index("rad")
     a = space // nj
@@ -123,70 +122,60 @@
     noting.wait()
     pl.semaphore_wait(barrier, group - 1 + na - 1)
 
-    lane128 = iota((1, 128), 1)
     left = iota((16, 128), 1) < QUARTER
-    tag = 128 // na
-
-    def outbound(dj, dy):
+    tagged = (iota((16, 128), 0) & 3) == 3
+    first = (iota((16, 128), 1) & HALO_DEV) == 0
+
+    def outbound(c, dj, dy):
         t = dj * ny + dy
         return pltpu.make_async_remote_copy(
-            src_ref=send.at[t], dst_ref=recv.at[me], send_sem=send1.at[t], recv_sem=recv1.at[me],
+            src_ref=send.at[c, t], dst_ref=recv.at[c, me], send_sem=send1.at[c], recv_sem=recv1.at[c],
             device_id=(a * nj + dj, dy), device_id_type=MESH)
 
-    def assemble(i, carry):
-        dj = lax.rem(j + 1 + i, nj)
-        labels = jnp.zeros((1, 128), F32)
-        for p in range(pairs):
-            codes = [code_s[0, 2 * p * nj + dj], code_s[0, (2 * p + 1) * nj + dj]]
-            held = [pieces[lax.shift_right_logical(jnp.maximum(c - 1, 0), 5)] for c in codes]
-            there = [jnp.where(c > 0, 1, 0) for c in codes]
+    def everyone(c):
+        return pltpu.make_async_remote_copy(
+            src_ref=send.at[c, pl.ds(0, group - 1)], dst_ref=recv.at[c, pl.ds(0, group - 1)],
+            send_sem=send1.at[c], recv_sem=recv1.at[c], device_id=(space, y), device_id_type=MESH)
+
+    def onward(i):
+        return pltpu.make_async_remote_copy(
+            src_ref=dense.at[i], dst_ref=got.at[i], send_sem=send2.at[i], recv_sem=recv2.at[i],
+            device_id=(lax.rem(a + i, na) * nj + j, y), device_id_type=MESH)
+
+    order = [(na // 2 + p, na // 2 - 1 - p) for p in range(pairs)]
+
+    for c, ahead in enumerate(order):
+        bases = [lax.rem(a + i, na) * nj for i in ahead]
+
+        def assemble(dj, carry):
+            codes = [code_s[0, base + dj] for base in bases]
+            held = [pieces[lax.shift_right_logical(jnp.maximum(code - 1, 0), 5)] for code in codes]
+            there = [jnp.where(code > 0, 1, 0) for code in codes]
+            ranks = [jnp.where(code > 0, (code - 1) & (HALO_DEV - 1), -1).astype(F32) for code in codes]
             both = jnp.where(left, held[0], held[1])
             both = jnp.where(jnp.where(left, there[0], there[1]) > 0, both, 0.0)
-            for par in range(2):
-                rank = jnp.where(codes[par] > 0, (codes[par] - 1) & (HALO_DEV - 1), -1).astype(F32)
-                labels = jnp.where(lane128 // tag == 2 * p + par, rank, labels)
+            both = jnp.where(tagged, jnp.where(first, ranks[0], ranks[1]), both)
             for q in range(ny):
-                send[dj * ny + q, 3 * p:3 * p + 3, :] = both[4 * q:4 * q + 3]
-        for q in range(ny):
-            send[dj * ny + q, rows - 1:rows, :] = labels
-        for dy in range(ny):
-            @pl.when(jnp.logical_or(dj != j, dy != y))
-            def _():
-                outbound(dj, dy).start()
-        return carry
-
-    lax.fori_loop(0, nj, assemble, 0)
-    recv[me] = send[me]
-
-    def inbound(t):
-        return pltpu.make_async_remote_copy(
-            src_ref=send.at[t], dst_ref=recv.at[t], send_sem=send1.at[t], recv_sem=recv1.at[t],
-            device_id=(a * nj + t // ny, lax.rem(t, ny)), device_id_type=MESH)
-
-    def arrive(i, carry):
-        inbound(lax.rem(me + group - i, group)).wait_recv()
-        return carry
-
-    lax.fori_loop(1, group, arrive, 0)
-
-    labels = recv[:, rows - 1, :].astype(BF16)
-    labels = jnp.concatenate([labels] * 3, axis=0)
-    spread = jnp.where(iota((na * HALO_DEV, 128), 1) == tag * (iota((na * HALO_DEV, 128), 0) // HALO_DEV), 1.0, 0.0).astype(BF16)
-    spread = nt(spread, labels)
-    wanted = (iota(spread.shape, 0) & (HALO_DEV - 1)).astype(F32)
-    chosen = jnp.where(spread == wanted, 1.0, 0.0).astype(BF16)
-
-    def onward(d):
-        return pltpu.make_async_remote_copy(
-            src_ref=dense.at[d], dst_ref=got.at[a], send_sem=send2.at[d], recv_sem=recv2.at[a],
-            device_id=(d * nj + j, y), device_id_type=MESH)
-
-    for p in range(pairs):
-        columns = [jnp.concatenate(split3(recv[:, 3 * p + f, :]), axis=0) for f in range(3)]
-        total = jnp.dot(chosen[2 * HALO_DEV * p:2 * HALO_DEV * (p + 1)], jnp.concatenate(columns, axis=1),
-                        preferred_element_type=F32)
-        for par in range(2):
-            d = 2 * p + par
+                send[c, dj * ny + q] = both[4 * q:4 * q + 4]
+            for dy in range(ny):
+                @pl.when(jnp.logical_or(dj != j, dy != y))
+                def _():
+                    outbound(c, dj, dy).start()
+            return carry
+
+        lax.fori_loop(0, nj, assemble, 0, unroll=2)
+        recv[c, me] = send[c, me]
+
+    wanted = (iota((group, 128), 1) & (HALO_DEV - 1)).astype(F32)
+    for c, ahead in enumerate(order):
+        everyone(c).wait_recv()
+        chosen = jnp.where(recv[c, :, 3, :] == wanted, 1.0, 0.0)
+        chosen = chosen.T[:2 * HALO_DEV].astype(BF16)
+        columns = [split3(recv[c, :, f, :]) for f in range(3)]
+        total = sum(
+            jnp.dot(chosen, jnp.concatenate([column[s] for column in columns], axis=1), preferred_element_type=F32)
+            for s in range(3))
+        for par, i in enumerate(ahead):
             for f in range(3):
                 top = total[32 * par:32 * par + 16, 128 * f:128 * f + 128]
                 bottom = total[32 * par + 16:32 * par + 32, 128 * f:128 * f + 128]
@@ -194,28 +183,16 @@
                     merged = jnp.where(left, top, pltpu.roll(bottom, QUARTER, 1))
                 else:
                     merged = jnp.where(left, pltpu.roll(top, QUARTER, 1), bottom)
-                dense[d, :, 128 * f:128 * f + 128] = merged
-
-            @pl.when(d != a)
-            def _():
-                onward(d).start()
-
-    keep = pltpu.make_async_copy(dense.at[a], got.at[a], own_sem)
-    keep.start()
+                (dense if i else got)[i, :, 128 * f:128 * f + 128] = merged
+            if i:
+                onward(i).start()
+
     for i in range(1, na):
-        t = lax.rem(a + i, na)
-        pltpu.make_async_remote_copy(
-            src_ref=dense.at[t], dst_ref=got.at[t], send_sem=send2.at[t], recv_sem=recv2.at[t],
-            device_id=(t * nj + j, y), device_id_type=MESH).wait_recv()
-    keep.wait()
-
-    def sent(i, carry):
-        inbound(lax.rem(me + i, group)).wait_send()
-        return carry
-
-    lax.fori_loop(1, group, sent, 0)
+        onward(i).wait_recv()
+    for c in range(pairs):
+        everyone(c).wait_send()
     for i in range(1, na):
-        onward(lax.rem(a + i, na)).wait_send()
+        onward(i).wait_send()
 
 
 def finish(na, got_ref, mass_ref, vol_ref, ent_ref, vel_ref):
@@ -237,7 +214,7 @@
     spaces, ny = mesh.shape["space"], mesh.shape["rad"]
     na = 8 if spaces == 128 else 2
     nj = spaces // na
-    group, rows = nj * ny, 3 * (na // 2) + 1
+    group, pairs = nj * ny, na // 2
 
     def body(cell_bin, cell_fields, tile_halo, halo_owner):
         vmem = pl.BlockSpec(memory_space=pltpu.VMEM)
@@ -246,9 +223,9 @@
         out = jax.ShapeDtypeStruct((HALO_DEV, QUARTER), F32)
         got = pl.pallas_call(
             functools.partial(kernel, na, nj, ny),
-            out_shape=jax.ShapeDtypeStruct((na, 16, 384), F32),
+            out_shape=pltpu.VMEM((na, 16, 384), F32),
             in_specs=[anywhere] * 4,
-            out_specs=anywhere,
+            out_specs=vmem,
             scratch_shapes=[
                 pltpu.SMEM(tile_halo.shape, jnp.int32),
                 pltpu.SMEM(halo_owner.shape, jnp.int32),
@@ -257,17 +234,17 @@
                 pltpu.VMEM((spaces // 2, 16, 128), F32),
                 pltpu.VMEM((8, spaces), jnp.int32),
                 pltpu.SMEM((8, spaces), jnp.int32),
-                pltpu.VMEM((group, rows, 128), F32),
-                pltpu.VMEM((group, rows, 128), F32),
+                pltpu.VMEM((pairs, group, 4, 128), F32),
+                pltpu.VMEM((pairs, group, 4, 128), F32),
                 pltpu.VMEM((na, 16, 384), F32),
-                dma((10,)), dma, dma((group,)), dma((group,)), dma((na,)), dma((na,)), dma,
+                dma((10,)), dma, dma((pairs,)), dma((pairs,)), dma((na,)), dma((na,)),
             ],
             compiler_params=pltpu.CompilerParams(collective_id=0, has_side_effects=True),
             name="profiles",
         )(tile_halo, halo_owner, cell_bin.reshape(-1, TILE), cell_fields)
         return pl.pallas_call(
             functools.partial(finish, na), out_shape=(out,) * 4, in_specs=[vmem], out_specs=(vmem,) * 4, name="finish",
-        )(got)
+        )(pltpu.with_memory_space_constraint(got, pltpu.VMEM))
 
     in_specs = (P(("space", "rad")), P(None, ("space", "rad")), P(("space", "rad")), P())
     out_specs = (P("space", "rad"),) * 4

time: 40.7 us -> 38.4 us (0.943)
  the two profiles are of different devices: /device:TPU:8 before, /device:TPU:1 now
where the time goes in v3:
time: 38.4 us; the launch traced here: 38.2 us
  Pallas kernels  37.6 us (98%)
  between operations  0.64 us (2%)
    pallas_call x1, Pallas kernels, body(): pl.pallas_call(functools.partial(kernel, na, nj, ny), out_shape=pltpu.VME...  36.9 us

profile of v3, /device:TPU:1, one launch (start us, length us, event | category | flops | bytes accessed | tf_op | source)
XLA Modules:
  0.0 38.2 jit_solution(9948659628950138147)
XLA Ops:
  0.6 36.9 %profiles.1.got_ref = f32[8,16,384]{2,1,0:T(8,128)S(1)} custom-call(s32[128]{0:T(128)} %halo_hbm.1, s32[4096]{0:T(1024)} %owner_hbm.1, s32[128,128]{1,0:T(8,128)} %bitcast.1, f32[3,16384]{1,0:T(4,128)} %fld_hbm.1), custom_call_target="tpu_custom_call" | custom-call | tf_op jit(solution)/shard_map/profiles/pallas_call | solution.py:224
  37.5 0.7 %finish.1 = (f32[32,64]{1,0:T(8,128)}, f32[32,64]{1,0:T(8,128)}, f32[32,64]{1,0:T(8,128)}, f32[32,64]{1,0:T(8,128)}) custom-call(f32[8,16,384]{2,1,0:T(8,128)S(1)} %profiles.1.got_ref), custom_call_target="tpu_custom_call" | custom-call | tf_op jit(solution)/shard_map/finish/pallas_call | solution.py:245

commit v4 on v3

--- a/solution.py
+++ b/solution.py
@@ -58,7 +58,7 @@
 
 
 def kernel(na, nj, ny, halo_hbm, owner_hbm, bin_hbm, fld_hbm, got, halo_ref, owner_ref, bin_ref, fld_ref,
-           pieces, code_v, code_s, send, recv, dense, in_sem, code_sem, send1, recv1, send2, recv2):
+           pieces, code_v, code_s, send, recv, dense, in_sem, code_sem, send1, recv1, send2, recv2, ready1, ready2):
     owners = na * nj
     count = owners // 2
     pairs = na // 2
@@ -82,13 +82,16 @@
         fetch.start()
 
     barrier = pltpu.get_barrier_semaphore()
-    for i in range(1, na):
-        pl.semaphore_signal(barrier, inc=1, device_id=(lax.rem(a + i, na) * nj + j, y), device_id_type=MESH)
-    for dj in range(nj):
+    core = lax.rem(space, 2)
+    sibling = space + 1 - 2 * core
+    for dj in range(0, nj, 2):
         for dy in range(ny):
             @pl.when(jnp.logical_or(dj != j, dy != y))
             def _():
                 pl.semaphore_signal(barrier, inc=1, device_id=(a * nj + dj, dy), device_id_type=MESH)
+    for i in range(1, na):
+        pl.semaphore_signal(
+            barrier, inc=1, device_id=(lax.rem(a + i, na) * nj + j + 1 - core, y), device_id_type=MESH)
 
     lane = iota((8, owners), 1)
 
@@ -120,7 +123,15 @@
         else:
             lax.fori_loop(size * c, size * (c + 1), one_piece, 0, unroll=size)
     noting.wait()
-    pl.semaphore_wait(barrier, group - 1 + na - 1)
+
+    @pl.when(core == 0)
+    def _():
+        pl.semaphore_wait(barrier, group - 1)
+        pl.semaphore_signal(ready1, inc=1, device_id=(sibling, y), device_id_type=MESH)
+
+    @pl.when(core == 1)
+    def _():
+        pl.semaphore_wait(ready1, 1)
 
     left = iota((16, 128), 1) < QUARTER
     tagged = (iota((16, 128), 0) & 3) == 3
@@ -184,6 +195,15 @@
                 else:
                     merged = jnp.where(left, pltpu.roll(top, QUARTER, 1), bottom)
                 (dense if i else got)[i, :, 128 * f:128 * f + 128] = merged
+            if i == order[0][0]:
+                @pl.when(core == 1)
+                def _():
+                    pl.semaphore_wait(barrier, 2 * (na - 1))
+                    pl.semaphore_signal(ready2, inc=1, device_id=(sibling, y), device_id_type=MESH)
+
+                @pl.when(core == 0)
+                def _():
+                    pl.semaphore_wait(ready2, 1)
             if i:
                 onward(i).start()
 
@@ -238,6 +258,7 @@
                 pltpu.VMEM((pairs, group, 4, 128), F32),
                 pltpu.VMEM((na, 16, 384), F32),
                 dma((10,)), dma, dma((pairs,)), dma((pairs,)), dma((na,)), dma((na,)),
+                pltpu.SemaphoreType.REGULAR, pltpu.SemaphoreType.REGULAR,
             ],
             compiler_params=pltpu.CompilerParams(collective_id=0, has_side_effects=True),
             name="profiles",

time: 38.4 us -> 35.3 us (0.919)
  the two profiles are of different devices: /device:TPU:1 before, /device:TPU:24 now
where the time goes in v4:
time: 35.3 us; the launch traced here: 35.1 us
  Pallas kernels  34.5 us (98%)
  between operations  0.64 us (2%)
    pallas_call x1, Pallas kernels, body(): pl.pallas_call(functools.partial(kernel, na, nj, ny), out_shape=pltpu.VME...  33.8 us

profile of v4, /device:TPU:24, one launch (start us, length us, event | category | flops | bytes accessed | tf_op | source)
XLA Modules:
  0.0 35.1 jit_solution(6524545878524665692)
XLA Ops:
  0.6 33.8 %profiles.1.got_ref = f32[8,16,384]{2,1,0:T(8,128)S(1)} custom-call(s32[128]{0:T(128)} %halo_hbm.1, s32[4096]{0:T(1024)} %owner_hbm.1, s32[128,128]{1,0:T(8,128)} %bitcast.1, f32[3,16384]{1,0:T(4,128)} %fld_hbm.1), custom_call_target="tpu_custom_call" | custom-call | tf_op jit(solution)/shard_map/profiles/pallas_call | solution.py:244
  34.4 0.7 %finish.1 = (f32[32,64]{1,0:T(8,128)}, f32[32,64]{1,0:T(8,128)}, f32[32,64]{1,0:T(8,128)}, f32[32,64]{1,0:T(8,128)}) custom-call(f32[8,16,384]{2,1,0:T(8,128)S(1)} %profiles.1.got_ref), custom_call_target="tpu_custom_call" | custom-call | tf_op jit(solution)/shard_map/finish/pallas_call | solution.py:266

commit v5 on v4

--- a/solution.py
+++ b/solution.py
@@ -81,6 +81,11 @@
     for fetch in fetches:
         fetch.start()
 
+    def across(t, dj):
+        d = lax.rem(t + na - a, na)
+        half = na // 2
+        return lax.rem(dj + (nj // 2) * (d // half) * (1 - (lax.rem(d, half) + half - 1) // half), nj)
+
     barrier = pltpu.get_barrier_semaphore()
     core = lax.rem(space, 2)
     sibling = space + 1 - 2 * core
@@ -90,8 +95,8 @@
             def _():
                 pl.semaphore_signal(barrier, inc=1, device_id=(a * nj + dj, dy), device_id_type=MESH)
     for i in range(1, na):
-        pl.semaphore_signal(
-            barrier, inc=1, device_id=(lax.rem(a + i, na) * nj + j + 1 - core, y), device_id_type=MESH)
+        t = lax.rem(a + i, na)
+        pl.semaphore_signal(barrier, inc=1, device_id=(t * nj + across(t, j) // 2 * 2 + 1, y), device_id_type=MESH)
 
     lane = iota((8, owners), 1)
 
@@ -148,18 +153,22 @@
             src_ref=send.at[c, pl.ds(0, group - 1)], dst_ref=recv.at[c, pl.ds(0, group - 1)],
             send_sem=send1.at[c], recv_sem=recv1.at[c], device_id=(space, y), device_id_type=MESH)
 
-    def onward(i):
+    def onward(t, slot):
         return pltpu.make_async_remote_copy(
-            src_ref=dense.at[i], dst_ref=got.at[i], send_sem=send2.at[i], recv_sem=recv2.at[i],
-            device_id=(lax.rem(a + i, na) * nj + j, y), device_id_type=MESH)
-
-    order = [(na // 2 + p, na // 2 - 1 - p) for p in range(pairs)]
-
-    for c, ahead in enumerate(order):
-        bases = [lax.rem(a + i, na) * nj for i in ahead]
-
-        def assemble(dj, carry):
-            codes = [code_s[0, base + dj] for base in bases]
+            src_ref=dense.at[t], dst_ref=got.at[slot], send_sem=send2.at[t], recv_sem=recv2.at[slot],
+            device_id=(t * nj + across(t, j), y), device_id_type=MESH)
+
+    order = [(2 * p, 2 * p + 1) for p in range(pairs)]
+    plane = nj // 4 if nj == 16 else 1
+
+    for c, targets in enumerate(order):
+
+        def assemble(k, turn):
+            if nj == 16:
+                dj = lax.rem(j // 2 + turn, 4) * 2 + (k // 2) * 8 + lax.rem(k, 2)
+            else:
+                dj = lax.rem(j + turn, nj)
+            codes = [code_s[0, t * nj + across(t, dj)] for t in targets]
             held = [pieces[lax.shift_right_logical(jnp.maximum(code - 1, 0), 5)] for code in codes]
             there = [jnp.where(code > 0, 1, 0) for code in codes]
             ranks = [jnp.where(code > 0, (code - 1) & (HALO_DEV - 1), -1).astype(F32) for code in codes]
@@ -168,17 +177,22 @@
             both = jnp.where(tagged, jnp.where(first, ranks[0], ranks[1]), both)
             for q in range(ny):
                 send[c, dj * ny + q] = both[4 * q:4 * q + 4]
-            for dy in range(ny):
-                @pl.when(jnp.logical_or(dj != j, dy != y))
-                def _():
+            for turn_y in (2, 1, 3, 0):
+                dy = lax.rem(y + turn_y, ny)
+                if turn_y:
                     outbound(c, dj, dy).start()
-            return carry
-
-        lax.fori_loop(0, nj, assemble, 0, unroll=2)
+                else:
+                    @pl.when(dj != j)
+                    def _():
+                        outbound(c, dj, dy).start()
+            return turn
+
+        for turn in (2, 1, 3, 0) if nj == 16 else range(nj):
+            lax.fori_loop(0, plane, assemble, turn, unroll=2)
         recv[c, me] = send[c, me]
 
     wanted = (iota((group, 128), 1) & (HALO_DEV - 1)).astype(F32)
-    for c, ahead in enumerate(order):
+    for c, targets in enumerate(order):
         everyone(c).wait_recv()
         chosen = jnp.where(recv[c, :, 3, :] == wanted, 1.0, 0.0)
         chosen = chosen.T[:2 * HALO_DEV].astype(BF16)
@@ -186,7 +200,7 @@
         total = sum(
             jnp.dot(chosen, jnp.concatenate([column[s] for column in columns], axis=1), preferred_element_type=F32)
             for s in range(3))
-        for par, i in enumerate(ahead):
+        for par, t in enumerate(targets):
             for f in range(3):
                 top = total[32 * par:32 * par + 16, 128 * f:128 * f + 128]
                 bottom = total[32 * par + 16:32 * par + 32, 128 * f:128 * f + 128]
@@ -194,8 +208,8 @@
                     merged = jnp.where(left, top, pltpu.roll(bottom, QUARTER, 1))
                 else:
                     merged = jnp.where(left, pltpu.roll(top, QUARTER, 1), bottom)
-                (dense if i else got)[i, :, 128 * f:128 * f + 128] = merged
-            if i == order[0][0]:
+                dense[t, :, 128 * f:128 * f + 128] = merged
+            if t == 0:
                 @pl.when(core == 1)
                 def _():
                     pl.semaphore_wait(barrier, 2 * (na - 1))
@@ -204,15 +218,20 @@
                 @pl.when(core == 0)
                 def _():
                     pl.semaphore_wait(ready2, 1)
-            if i:
-                onward(i).start()
-
+
+            @pl.when(t != a)
+            def _():
+                onward(t, a).start()
+
+    got[a] = dense[a]
     for i in range(1, na):
-        onward(i).wait_recv()
+        t = lax.rem(a + i, na)
+        onward(t, t).wait_recv()
     for c in range(pairs):
         everyone(c).wait_send()
     for i in range(1, na):
-        onward(i).wait_send()
+        t = lax.rem(a + i, na)
+        onward(t, t).wait_send()
 
 
 def finish(na, got_ref, mass_ref, vol_ref, ent_ref, vel_ref):

time: 35.3 us -> 34.1 us (0.966)
  the two profiles are of different devices: /device:TPU:24 before, /device:TPU:64 now
where the time goes in v5:
time: 34.1 us; the launch traced here: 33.9 us
  Pallas kernels  33.3 us (98%)
  between operations  0.64 us (2%)
    pallas_call x1, Pallas kernels, body(): pl.pallas_call(functools.partial(kernel, na, nj, ny), out_shape=pltpu.VME...  32.6 us
    pallas_call x1, Pallas kernels, body(): pl.pallas_call(functools.partial(finish, na), out_shape=(out,) * 4, in_sp...  0.7 us

profile of v5, /device:TPU:64, one launch (start us, length us, event | category | flops | bytes accessed | tf_op | source)
XLA Modules:
  0.0 33.9 jit_solution(18403030119615601401)
XLA Ops:
  0.6 32.6 %profiles.1.got_ref = f32[8,16,384]{2,1,0:T(8,128)S(1)} custom-call(s32[128]{0:T(128)} %halo_hbm.1, s32[4096]{0:T(1024)} %owner_hbm.1, s32[128,128]{1,0:T(8,128)} %bitcast.1, f32[3,16384]{1,0:T(4,128)} %fld_hbm.1), custom_call_target="tpu_custom_call" | custom-call | tf_op jit(solution)/shard_map/profiles/pallas_call | solution.py:263
  33.2 0.7 %finish.1 = (f32[32,64]{1,0:T(8,128)}, f32[32,64]{1,0:T(8,128)}, f32[32,64]{1,0:T(8,128)}, f32[32,64]{1,0:T(8,128)}) custom-call(f32[8,16,384]{2,1,0:T(8,128)S(1)} %profiles.1.got_ref), custom_call_target="tpu_custom_call" | custom-call | tf_op jit(solution)/shard_map/finish/pallas_call | solution.py:285

commit v6 on v5

v6 whole, which is shorter than its diff:
```python
import functools

import jax
import jax.numpy as jnp
from jax import lax
from jax.experimental import pallas as pl
from jax.experimental.pallas import tpu as pltpu
from jax.sharding import PartitionSpec as P

MESH = pl.DeviceIdType.MESH
F32 = jnp.float32
BF16 = jnp.bfloat16
TILE = 128
BINS = 256
QUARTER = 64
HALO_DEV = 32
log_inner = -2.302585092994046
AHEAD = 3


def halves(v):
    high = v.astype(BF16).astype(F32)
    return high, v - high


def iota(shape, dim):
    return lax.broadcasted_iota(jnp.int32, shape, dim)


def nt(a, b):
    return lax.dot_general(a, b, (((1,), (1,)), ((), ())), preferred_element_type=F32)


def bin_piece(k, bin_ref, fld_ref):
    label = jnp.concatenate([bin_ref[pl.ds(2 * k, 1), :], bin_ref[pl.ds(2 * k + 1, 1), :]], axis=1)
    low = label & (QUARTER - 1)
    high = lax.shift_right_logical(label, 6)
    v = fld_ref[:, pl.ds(pl.multiple_of(2 * TILE * k, 2 * TILE), 2 * TILE)]
    pad = jnp.zeros((1, 2 * TILE), F32)
    v8 = jnp.concatenate([v, pad, v, pad], axis=0)
    row = iota((8, 2 * TILE), 0)
    quarters = [2 * t + lax.shift_right_logical(row, 2) for t in range(2)]
    lhs = jnp.concatenate([jnp.where(high == q, part, 0.0) for part in halves(v8) for q in quarters], axis=0)
    bases = [jnp.sum(jnp.where(high < q, v8, 0.0), axis=1, keepdims=True) for q in quarters]
    below = jnp.where(low <= iota((QUARTER, 2 * TILE), 0), 1.0, 0.0).astype(BF16)
    below = jnp.concatenate([below, below], axis=0)
    out = nt(lhs.astype(BF16), below)
    return out[0:16] + out[16:32] + jnp.concatenate(bases, axis=0)


def kernel(na, nj, ny, halo_hbm, owner_hbm, bin_hbm, fld_hbm, sums, halo_ref, owner_ref, bin_ref, fld_ref,
           pieces, code_v, code_s, send_first, recv_first, send_rest, recv_rest, dense, got, in_sem, code_sem, send1, recv1, send2, recv2, ready1, ready2):
    owners = na * nj
    count = owners // 2
    pairs = na // 2
    group = nj * ny
    space = lax.axis_index("space")
    y = lax.axis_index("rad")
    a = space // nj
    j = space % nj
    me = j * ny + y

    chunks = min(2, count)
    size = count // chunks
    fetches = [pltpu.make_async_copy(halo_hbm, halo_ref, in_sem.at[0]),
               pltpu.make_async_copy(owner_hbm, owner_ref, in_sem.at[1])]
    for c in range(chunks):
        fetches.append(pltpu.make_async_copy(
            bin_hbm.at[2 * size * c:2 * size * (c + 1)], bin_ref.at[2 * size * c:2 * size * (c + 1)], in_sem.at[2 + 2 * c]))
        cells = slice(2 * TILE * size * c, 2 * TILE * size * (c + 1))
        fetches.append(pltpu.make_async_copy(fld_hbm.at[:, cells], fld_ref.at[:, cells], in_sem.at[3 + 2 * c]))
    for fetch in fetches:
        fetch.start()

    def across(t, dj):
        d = lax.rem(t + na - a, na)
        half = na // 2
        return lax.rem(dj + (nj // 2) * (d // half) * (1 - (lax.rem(d, half) + half - 1) // half), nj)

    barrier = pltpu.get_barrier_semaphore()
    core = lax.rem(space, 2)
    sibling = space + 1 - 2 * core
    for dj in range(0, nj, 2):
        for dy in range(ny):
            @pl.when(jnp.logical_or(dj != j, dy != y))
            def _():
                pl.semaphore_signal(barrier, inc=1, device_id=(a * nj + dj, dy), device_id_type=MESH)
    for i in range(1, na):
        t = lax.rem(a + i, na)
        pl.semaphore_signal(barrier, inc=1, device_id=(t * nj + across(t, j) // 2 * 2 + 1, y), device_id_type=MESH)

    lane = iota((8, owners), 1)

    def note(k, codes):
        halo = halo_ref[2 * k]
        code = HALO_DEV * k + (halo & (HALO_DEV - 1))
        return jnp.where(lane == owner_ref[halo], code, codes)

    def piece_and_notes(k, codes):
        pieces[k] = bin_piece(k, bin_ref, fld_ref)
        return note(2 * k + 1, note(2 * k, codes))

    def one_piece(k, carry):
        pieces[k] = bin_piece(k, bin_ref, fld_ref)
        return carry

    noting = pltpu.make_async_copy(code_v, code_s, code_sem)
    fetches[0].wait()
    fetches[1].wait()
    codes = jnp.full((8, owners), HALO_DEV * count, jnp.int32)
    pieces[count] = jnp.zeros((16, 128), F32)
    for c in range(chunks):
        fetches[2 + 2 * c].wait()
        fetches[3 + 2 * c].wait()
        if 2 * c < chunks:
            codes = lax.fori_loop(size * c, size * (c + 1), piece_and_notes, codes, unroll=size)
            if 2 * (c + 1) == chunks:
                code_v[...] = codes
                noting.start()
        else:
            lax.fori_loop(size * c, size * (c + 1), one_piece, 0, unroll=size)
    noting.wait()

    @pl.when(core == 0)
    def _():
        pl.semaphore_wait(barrier, group - 1)
        pl.semaphore_signal(ready1, inc=1, device_id=(sibling, y), device_id_type=MESH)

    @pl.when(core == 1)
    def _():
        pl.semaphore_wait(ready1, 1)

    left = iota((16, 128), 1) < QUARTER
    tagged = (iota((16, 128), 0) & 3) == 3
    block = lax.shift_right_logical(iota((8, 128), 1), 4)
    send = [send_first] + [send_rest.at[c] for c in range(pairs - 1)]
    recv = [recv_first] + [recv_rest.at[c] for c in range(pairs - 1)]

    def outbound(c, dj, dy):
        t = dj * ny + dy
        return pltpu.make_async_remote_copy(
            src_ref=send[c].at[t], dst_ref=recv[c].at[me], send_sem=send1.at[c], recv_sem=recv1.at[c],
            device_id=(a * nj + dj, dy), device_id_type=MESH)

    def everyone(c):
        return pltpu.make_async_remote_copy(
            src_ref=send[c].at[pl.ds(0, group - 1)], dst_ref=recv[c].at[pl.ds(0, group - 1)],
            send_sem=send1.at[c], recv_sem=recv1.at[c], device_id=(space, y), device_id_type=MESH)

    def onward(t, slot):
        return pltpu.make_async_remote_copy(
            src_ref=dense.at[t], dst_ref=got.at[slot], send_sem=send2.at[t], recv_sem=recv2.at[slot],
            device_id=(t * nj + across(t, j), y), device_id_type=MESH)

    order = [(2 * p, 2 * p + 1) for p in range(pairs)]

    def dispatch(c):
        for turn in (2, 1, 3, 0) if nj == 16 else range(nj):
            if nj == 16:
                dests = [lax.rem(j // 2 + turn, 4) * 2 + 8 * (k % 2) + k // 2 for k in range(4)]
            else:
                dests = [lax.rem(j + turn, nj)]
            for dj in dests:
                codes = [code_s[0, t * nj + across(t, dj)] for t in order[c]]
                held = [pieces[lax.shift_right_logical(code, 5)] for code in codes]
                both = jnp.where(left, held[0], held[1])
                if c == 0:
                    ranks = jnp.zeros((8, 128), jnp.int32)
                    for n, t in enumerate(sum(order, ())):
                        rank = code_s[0, t * nj + across(t, dj)] & (HALO_DEV - 1)
                        ranks = jnp.where(block == n, rank, ranks)
                    ranks = ranks.astype(F32)
                    both = jnp.where(tagged, jnp.concatenate([ranks, ranks], axis=0), both)
                for q in range(ny):
                    send[c][dj * ny + q] = both[4 * q:4 * q + (3 if c else 4)]
            for dj in dests:
                for turn_y in (2, 1, 3, 0):
                    dy = lax.rem(y + turn_y, ny)
                    if turn or turn_y:
                        outbound(c, dj, dy).start()
                    else:
                        @pl.when(dj != j)
                        def _():
                            outbound(c, dj, dy).start()
        recv[c][me] = send[c][me]

    for c in range(min(AHEAD, pairs)):
        dispatch(c)

    @pl.when(core == 1)
    def _():
        pl.semaphore_wait(barrier, 2 * (na - 1))
        pl.semaphore_signal(ready2, inc=1, device_id=(sibling, y), device_id_type=MESH)

    for c, targets in enumerate(order):
        everyone(c).wait_recv()
        if c == 0:
            labels = recv_first[:, 3, :]
            wanted = lax.rem(iota((group, 128), 1), 16)
            chosen = [jnp.where(labels == (wanted + 16 * half).astype(F32), 1.0, 0.0).T.astype(BF16) for half in range(2)]
        lhs = jnp.concatenate([rows[32 * c:32 * (c + 1)] for rows in chosen], axis=0)
        columns = [halves(recv[c][:, f, :]) for f in range(3)]
        total = sum(
            jnp.dot(lhs, jnp.concatenate([column[s] for column in columns], axis=1).astype(BF16), preferred_element_type=F32)
            for s in range(2))
        for par, t in enumerate(targets):
            for f in range(3):
                top = total[16 * par:16 * par + 16, 128 * f:128 * f + 128]
                bottom = total[16 * par + 32:16 * par + 48, 128 * f:128 * f + 128]
                if par == 0:
                    merged = jnp.where(left, top, pltpu.roll(bottom, QUARTER, 1))
                else:
                    merged = jnp.where(left, pltpu.roll(top, QUARTER, 1), bottom)
                dense[t, :, 128 * f:128 * f + 128] = merged
            if c == 0 and par == 0:
                @pl.when(core == 0)
                def _():
                    pl.semaphore_wait(ready2, 1)

            @pl.when(t != a)
            def _():
                onward(t, a).start()

        if c + AHEAD < pairs:
            dispatch(c + AHEAD)

    for c in range(pairs):
        everyone(c).wait_send()
    for i in range(1, na):
        t = lax.rem(a + i, na)
        onward(t, t).wait_send()
    total = dense[a]
    for i in range(1, na):
        t = lax.rem(a + i, na)
        onward(t, t).wait_recv()
        total = total + got[t]
    sums[...] = total


def finish(sums_ref, mass_ref, vol_ref, ent_ref, vel_ref):
    total = sums_ref[...]
    bins = (lax.axis_index("rad") * QUARTER + 1 + iota((16, QUARTER), 1)).astype(F32)
    radius = jnp.exp(log_inner + bins * (-log_inner / BINS))
    for f, ref in enumerate((mass_ref, vol_ref, ent_ref)):
        block = total[:, 128 * f:128 * f + 128]
        for half, part in enumerate((block, pltpu.roll(block, QUARTER, 1))):
            part = part[:, :QUARTER]
            ref[16 * half:16 * half + 16, :] = part
            if f == 0:
                vel_ref[16 * half:16 * half + 16, :] = jnp.sqrt(part / radius)


def solution(mesh):
    spaces, ny = mesh.shape["space"], mesh.shape["rad"]
    na = 8 if spaces == 128 else 2
    nj = spaces // na
    group, pairs = nj * ny, na // 2

    def body(cell_bin, cell_fields, tile_halo, halo_owner):
        vmem = pl.BlockSpec(memory_space=pltpu.VMEM)
        anywhere = pl.BlockSpec(memory_space=pl.ANY)
        dma = pltpu.SemaphoreType.DMA
        out = jax.ShapeDtypeStruct((HALO_DEV, QUARTER), F32)
        sums = pl.pallas_call(
            functools.partial(kernel, na, nj, ny),
            out_shape=pltpu.VMEM((16, 384), F32),
            in_specs=[anywhere] * 4,
            out_specs=vmem,
            scratch_shapes=[
                pltpu.SMEM(tile_halo.shape, jnp.int32),
                pltpu.SMEM(halo_owner.shape, jnp.int32),
                pltpu.VMEM((tile_halo.shape[0], TILE), jnp.int32),
                pltpu.VMEM(cell_fields.shape, F32),
                pltpu.VMEM((spaces // 2 + 1, 16, 128), F32),
                pltpu.VMEM((8, spaces), jnp.int32),
                pltpu.SMEM((8, spaces), jnp.int32),
                pltpu.VMEM((group, 4, 128), F32),
                pltpu.VMEM((group, 4, 128), F32),
                pltpu.VMEM((max(pairs - 1, 1), group, 3, 128), F32),
                pltpu.VMEM((max(pairs - 1, 1), group, 3, 128), F32),
                pltpu.VMEM((na, 16, 384), F32),
                pltpu.VMEM((na, 16, 384), F32),
                dma((10,)), dma, dma((pairs,)), dma((pairs,)), dma((na,)), dma((na,)),
                pltpu.SemaphoreType.REGULAR, pltpu.SemaphoreType.REGULAR,
            ],
            compiler_params=pltpu.CompilerParams(collective_id=0, has_side_effects=True),
            name="profiles",
        )(tile_halo, halo_owner, cell_bin.reshape(-1, TILE), cell_fields)
        return pl.pallas_call(
            finish, out_shape=(out,) * 4, in_specs=[vmem], out_specs=(vmem,) * 4, name="finish",
        )(pltpu.with_memory_space_constraint(sums, pltpu.VMEM))

    in_specs = (P(("space", "rad")), P(None, ("space", "rad")), P(("space", "rad")), P())
    out_specs = (P("space", "rad"),) * 4
    return jax.shard_map(body, mesh=mesh, in_specs=in_specs, out_specs=out_specs, check_vma=False)
```

time: 34.1 us -> 31.9 us (0.935)
  the two profiles are of different devices: /device:TPU:64 before, /device:TPU:448 now
where the time goes in v6:
time: 31.9 us; the launch traced here: 31.7 us
  Pallas kernels  31.1 us (97%)
  between operations  0.64 us (2%)
    pallas_call x1, Pallas kernels, body(): pl.pallas_call(functools.partial(kernel, na, nj, ny), out_shape=pltpu.VME...  30.4 us
    pallas_call x1, Pallas kernels, body(): pl.pallas_call(finish, out_shape=(out,) * 4, in_specs=[vmem], out_specs=(...  0.69 us

profile of v6, /device:TPU:448, one launch (start us, length us, event | category | flops | bytes accessed | tf_op | source)
XLA Modules:
  0.0 31.7 jit_solution(5855134323004969619)
XLA Ops:
  0.6 30.4 %profiles.1.sums_ref = f32[16,384]{1,0:T(8,128)S(1)} custom-call(s32[128]{0:T(128)} %halo_hbm.1, s32[4096]{0:T(1024)} %owner_hbm.1, s32[128,128]{1,0:T(8,128)} %bitcast.1, f32[3,16384]{1,0:T(4,128)} %fld_hbm.1), custom_call_target="tpu_custom_call" | custom-call | tf_op jit(solution)/shard_map/profiles/pallas_call | solution.py:264
  31.0 0.7 %finish.1 = (f32[32,64]{1,0:T(8,128)}, f32[32,64]{1,0:T(8,128)}, f32[32,64]{1,0:T(8,128)}, f32[32,64]{1,0:T(8,128)}) custom-call(f32[16,384]{1,0:T(8,128)S(1)} %profiles.1.sums_ref), custom_call_target="tpu_custom_call" | custom-call | tf_op jit(solution)/shard_map/finish/pallas_call | solution.py:289

commit v7 on v6

--- a/solution.py
+++ b/solution.py
@@ -15,7 +15,6 @@
 QUARTER = 64
 HALO_DEV = 32
 log_inner = -2.302585092994046
-AHEAD = 3
 
 
 def halves(v):
@@ -72,22 +71,23 @@
     for fetch in fetches:
         fetch.start()
 
-    def across(t, dj):
-        d = lax.rem(t + na - a, na)
-        half = na // 2
-        return lax.rem(dj + (nj // 2) * (d // half) * (1 - (lax.rem(d, half) + half - 1) // half), nj)
-
     barrier = pltpu.get_barrier_semaphore()
     core = lax.rem(space, 2)
     sibling = space + 1 - 2 * core
-    for dj in range(0, nj, 2):
-        for dy in range(ny):
-            @pl.when(jnp.logical_or(dj != j, dy != y))
-            def _():
-                pl.semaphore_signal(barrier, inc=1, device_id=(a * nj + dj, dy), device_id_type=MESH)
+    for turn in (2, 1, 3, 0) if nj == 16 else (0,):
+        for b in range(2 if nj == 16 else 1):
+            dj = lax.rem(j // 2 + turn, 4) * 2 + 8 * b if nj == 16 else 0
+            for turn_y in (2, 1, 3, 0):
+                dy = lax.rem(y + turn_y, ny)
+                if turn or turn_y:
+                    pl.semaphore_signal(barrier, inc=1, device_id=(a * nj + dj, dy), device_id_type=MESH)
+                else:
+                    @pl.when(dj != j)
+                    def _():
+                        pl.semaphore_signal(barrier, inc=1, device_id=(a * nj + dj, dy), device_id_type=MESH)
     for i in range(1, na):
         t = lax.rem(a + i, na)
-        pl.semaphore_signal(barrier, inc=1, device_id=(t * nj + across(t, j) // 2 * 2 + 1, y), device_id_type=MESH)
+        pl.semaphore_signal(barrier, inc=1, device_id=(t * nj + j // 2 * 2 + 1, y), device_id_type=MESH)
 
     lane = iota((8, owners), 1)
 
@@ -150,9 +150,10 @@
     def onward(t, slot):
         return pltpu.make_async_remote_copy(
             src_ref=dense.at[t], dst_ref=got.at[slot], send_sem=send2.at[t], recv_sem=recv2.at[slot],
-            device_id=(t * nj + across(t, j), y), device_id_type=MESH)
-
-    order = [(2 * p, 2 * p + 1) for p in range(pairs)]
+            device_id=(t * nj + j, y), device_id_type=MESH)
+
+    turned = [2 * (p + 1 - 2 * (p % 2)) if nj == 16 and 2 * p >= pairs else 2 * p for p in range(pairs)]
+    orders = [[(2 * p, 2 * p + 1) for p in range(pairs)], [(p, p + 1) for p in turned]]
 
     def dispatch(c):
         for turn in (2, 1, 3, 0) if nj == 16 else range(nj):
@@ -160,14 +161,15 @@
                 dests = [lax.rem(j // 2 + turn, 4) * 2 + 8 * (k % 2) + k // 2 for k in range(4)]
             else:
                 dests = [lax.rem(j + turn, nj)]
-            for dj in dests:
-                codes = [code_s[0, t * nj + across(t, dj)] for t in order[c]]
+            for k, dj in enumerate(dests):
+                order = orders[k // 2]
+                codes = [code_s[0, t * nj + dj] for t in order[c]]
                 held = [pieces[lax.shift_right_logical(code, 5)] for code in codes]
                 both = jnp.where(left, held[0], held[1])
                 if c == 0:
                     ranks = jnp.zeros((8, 128), jnp.int32)
                     for n, t in enumerate(sum(order, ())):
-                        rank = code_s[0, t * nj + across(t, dj)] & (HALO_DEV - 1)
+                        rank = code_s[0, t * nj + dj] & (HALO_DEV - 1)
                         ranks = jnp.where(block == n, rank, ranks)
                     ranks = ranks.astype(F32)
                     both = jnp.where(tagged, jnp.concatenate([ranks, ranks], axis=0), both)
@@ -184,7 +186,7 @@
                             outbound(c, dj, dy).start()
         recv[c][me] = send[c][me]
 
-    for c in range(min(AHEAD, pairs)):
+    for c in range(pairs):
         dispatch(c)
 
     @pl.when(core == 1)
@@ -192,7 +194,8 @@
         pl.semaphore_wait(barrier, 2 * (na - 1))
         pl.semaphore_signal(ready2, inc=1, device_id=(sibling, y), device_id_type=MESH)
 
-    for c, targets in enumerate(order):
+    for c in range(pairs):
+        targets = [orders[0][c][par] + core * (orders[1][c][par] - orders[0][c][par]) for par in range(2)]
         everyone(c).wait_recv()
         if c == 0:
             labels = recv_first[:, 3, :]
@@ -220,9 +223,6 @@
             @pl.when(t != a)
             def _():
                 onward(t, a).start()
-
-        if c + AHEAD < pairs:
-            dispatch(c + AHEAD)
 
     for c in range(pairs):
         everyone(c).wait_send()

time: 31.9 us -> 31.3 us (0.981)
  the two profiles are of different devices: /device:TPU:448 before, /device:TPU:70 now
where the time goes in v7:
time: 31.3 us; the launch traced here: 31.1 us
  Pallas kernels  30.5 us (97%)
  between operations  0.64 us (2%)
    pallas_call x1, Pallas kernels, body(): pl.pallas_call(functools.partial(kernel, na, nj, ny), out_shape=pltpu.VME...  29.8 us
    pallas_call x1, Pallas kernels, body(): pl.pallas_call(finish, out_shape=(out,) * 4, in_specs=[vmem], out_specs=(...  0.69 us

profile of v7, /device:TPU:70, one launch (start us, length us, event | category | flops | bytes accessed | tf_op | source)
XLA Modules:
  0.0 31.1 jit_solution(11952217136283618060)
XLA Ops:
  0.6 29.8 %profiles.1.sums_ref = f32[16,384]{1,0:T(8,128)S(1)} custom-call(s32[128]{0:T(128)} %halo_hbm.1, s32[4096]{0:T(1024)} %owner_hbm.1, s32[128,128]{1,0:T(8,128)} %bitcast.1, f32[3,16384]{1,0:T(4,128)} %fld_hbm.1), custom_call_target="tpu_custom_call" | custom-call | tf_op jit(solution)/shard_map/profiles/pallas_call | solution.py:264
  30.4 0.7 %finish.1 = (f32[32,64]{1,0:T(8,128)}, f32[32,64]{1,0:T(8,128)}, f32[32,64]{1,0:T(8,128)}, f32[32,64]{1,0:T(8,128)}) custom-call(f32[16,384]{1,0:T(8,128)S(1)} %profiles.1.sums_ref), custom_call_target="tpu_custom_call" | custom-call | tf_op jit(solution)/shard_map/finish/pallas_call | solution.py:289

commit v8 on v7

--- a/solution.py
+++ b/solution.py
@@ -198,14 +198,13 @@
         targets = [orders[0][c][par] + core * (orders[1][c][par] - orders[0][c][par]) for par in range(2)]
         everyone(c).wait_recv()
         if c == 0:
-            labels = recv_first[:, 3, :]
-            wanted = lax.rem(iota((group, 128), 1), 16)
-            chosen = [jnp.where(labels == (wanted + 16 * half).astype(F32), 1.0, 0.0).T.astype(BF16) for half in range(2)]
+            labels = recv_first[:, 3, :].T
+            wanted = iota((128, group), 0) & 15
+            chosen = [jnp.where(labels == (wanted + 16 * half).astype(F32), 1.0, 0.0).astype(BF16) for half in range(2)]
         lhs = jnp.concatenate([rows[32 * c:32 * (c + 1)] for rows in chosen], axis=0)
-        columns = [halves(recv[c][:, f, :]) for f in range(3)]
-        total = sum(
-            jnp.dot(lhs, jnp.concatenate([column[s] for column in columns], axis=1).astype(BF16), preferred_element_type=F32)
-            for s in range(2))
+        columns = [jnp.concatenate(halves(recv[c][:, f, :]), axis=0) for f in range(3)]
+        total = jnp.dot(
+            jnp.concatenate([lhs, lhs], axis=1), jnp.concatenate(columns, axis=1).astype(BF16), preferred_element_type=F32)
         for par, t in enumerate(targets):
             for f in range(3):
                 top = total[16 * par:16 * par + 16, 128 * f:128 * f + 128]

time: 31.3 us -> 31.2 us (level)
  no operation moved by 1% of the time
where the time goes in v8:
time: 31.2 us; the launch traced here: 31 us
  Pallas kernels  30.4 us (97%)
  between operations  0.64 us (2%)
    pallas_call x1, Pallas kernels, body(): pl.pallas_call(functools.partial(kernel, na, nj, ny), out_shape=pltpu.VME...  29.7 us
    pallas_call x1, Pallas kernels, body(): pl.pallas_call(finish, out_shape=(out,) * 4, in_specs=[vmem], out_specs=(...  0.69 us

profile of v8, /device:TPU:70, one launch (start us, length us, event | category | flops | bytes accessed | tf_op | source)
XLA Modules:
  0.0 31.0 jit_solution(11990185122286252582)
XLA Ops:
  0.6 29.7 %profiles.1.sums_ref = f32[16,384]{1,0:T(8,128)S(1)} custom-call(s32[128]{0:T(128)} %halo_hbm.1, s32[4096]{0:T(1024)} %owner_hbm.1, s32[128,128]{1,0:T(8,128)} %bitcast.1, f32[3,16384]{1,0:T(4,128)} %fld_hbm.1), custom_call_target="tpu_custom_call" | custom-call | tf_op jit(solution)/shard_map/profiles/pallas_call | solution.py:263
  30.3 0.7 %finish.1 = (f32[32,64]{1,0:T(8,128)}, f32[32,64]{1,0:T(8,128)}, f32[32,64]{1,0:T(8,128)}, f32[32,64]{1,0:T(8,128)}) custom-call(f32[16,384]{1,0:T(8,128)S(1)} %profiles.1.sums_ref), custom_call_target="tpu_custom_call" | custom-call | tf_op jit(solution)/shard_map/finish/pallas_call | solution.py:288
